TPU v7x, 32 devices: a whole 2x2x4 slice. The times are simulated.
32 devices in a mesh: rows: 8 (over y, x, core), cols: 4 (over z).
Axes of the slice: x: 2, y: 2, z: 4, core: 2. Of those that a mesh axis runs over, the one named last changes fastest.
Arguments:
- memory: float32 [128, 262144], P('cols', 'rows'), may hold values from -3 to 3
- last_tick: int32 [262144], P('rows'), may hold values from 0 to 999
- slot_node: int32 [64, 256], P('rows'), may hold values from 0 to 262143, as said below
- slot_pair: int32 [64, 256], P('rows'), may hold values from 0 to 2047, as said below
- slot_tick: int32 [64, 256], P('rows'), may hold values from 1000 to 1999
- block_count: int32 [8, 8], P('rows'), may hold values from 0 to 256, as said below
- time_freq: float32 [128], replicated, may hold values from 0.002 to 0.1
- time_phase: float32 [128], replicated, may hold values from -3.140625 to 3.140625
- w_pair: bfloat16 [128, 2, 384], P('cols'), may hold values from -0.3125 to 0.3125
- w_time: bfloat16 [128, 384], P('cols'), may hold values from -0.3125 to 0.3125
- w_hidden: bfloat16 [128, 384], P('cols'), may hold values from -0.5 to 0.5
- bias_input: float32 [384], P('cols'), may hold values from -3 to 3
- bias_hidden: float32 [384], P('cols'), may hold values from -3 to 3
Outputs:
- new_memory: float32 [128, 262144], P('cols', 'rows')
Inputs may be any that keep to these rules, and one draw needn't show every extreme that they name: `slot_node`: every slot of block b (live or not) names a node of owner b, from b * 32768 to (b + 1) * 32768 - 1. `slot_pair`: indexes the holder's 8 * 256 slots flattened block by block; the relation is symmetric without fixed points, and live slots pair with live slots. `block_count`: every count is even; in every draw one owner's block is full (256 live slots) from every holder.
All inputs are finite; a program needn't handle non-finite values.
Results may differ from a plain program's by a relative error of at most 0.0006.
Values may be sent and summed in bfloat16 or wider, within the bound.
A program may use at most 128 MiB of HBM per device.

v0:
```python
import math

import jax
import jax.numpy as jnp
from jax import lax
from jax.sharding import PartitionSpec as P


def node_means(ids, gate_in):
    total = ids.shape[0]
    step_rows = math.gcd(total, 512)
    turns = total // step_rows

    def one_block(index):
        mine = lax.dynamic_slice_in_dim(ids, index * step_rows, step_rows, 0)
        equal = (mine[:, None] == ids[None, :]).astype(jnp.float32)
        sums = jnp.dot(
            equal, gate_in, precision=lax.Precision.HIGHEST, preferred_element_type=jnp.float32
        )
        counts = jnp.sum(equal, axis=1)
        return sums / counts[:, None]

    blocks_out = lax.map(one_block, jnp.arange(turns, dtype=jnp.int32))
    return blocks_out.reshape(total, gate_in.shape[1])


def local(
    memory,
    last_tick,
    slot_node,
    slot_pair,
    slot_tick,
    block_count,
    time_freq,
    time_phase,
    w_pair,
    w_time,
    w_hidden,
    bias_input,
    bias_hidden,
):
    width_part, node_rows = memory.shape
    blocks, capacity = slot_node.shape
    column = lax.axis_index("cols")
    mem_rows = memory.T
    block_iota = lax.broadcasted_iota(jnp.int32, (blocks, capacity), 0)
    slot_iota = lax.broadcasted_iota(jnp.int32, (blocks, capacity), 1)
    filled = slot_iota < block_count.reshape(blocks, 1)
    local_ids = jnp.where(filled, slot_node - block_iota * node_rows, node_rows)
    asked, asked_tick = (
        lax.all_to_all(local_ids, "rows", split_axis=0, concat_axis=0, tiled=True),
        lax.all_to_all(slot_tick, "rows", split_axis=0, concat_axis=0, tiled=True),
    )
    safe_ids = jnp.minimum(asked, node_rows - 1)
    own_rows = mem_rows[safe_ids]
    own_gaps = (asked_tick - last_tick[safe_ids]).astype(jnp.float32)
    full_pair, full_time, full_hidden = (
        lax.all_gather(w_pair, "cols", axis=0, tiled=True),
        lax.all_gather(w_time, "cols", axis=0, tiled=True),
        lax.all_gather(w_hidden, "cols", axis=0, tiled=True),
    )
    start = column * 3 * width_part
    pick_pair = lax.dynamic_slice_in_dim(full_pair, start, 3 * width_part, 2)
    pick_time = lax.dynamic_slice_in_dim(full_time, start, 3 * width_part, 1)
    pick_hidden = lax.dynamic_slice_in_dim(full_hidden, start, 3 * width_part, 1)
    total = blocks * capacity
    replied = lax.all_to_all(
        own_rows.astype(jnp.bfloat16), "rows", split_axis=0, concat_axis=0, tiled=True
    )
    held_rows = replied.reshape(total, width_part)
    partner_rows = held_rows[slot_pair.reshape(-1)].reshape(blocks, capacity, width_part)
    arrived = lax.all_to_all(partner_rows, "rows", split_axis=0, concat_axis=0, tiled=True)
    self_full = lax.all_gather(
        own_rows.reshape(total, width_part).astype(jnp.bfloat16), "cols", axis=1, tiled=True
    )
    partner_full = lax.all_gather(arrived.reshape(total, width_part), "cols", axis=1, tiled=True)
    encoded = jnp.cos(
        own_gaps.reshape(-1)[:, None] * time_freq[None, :] + time_phase[None, :]
    ).astype(jnp.bfloat16)
    gate_in = jnp.dot(self_full, pick_pair[:, 0, :], preferred_element_type=jnp.float32)
    gate_in = gate_in + jnp.dot(
        partner_full, pick_pair[:, 1, :], preferred_element_type=jnp.float32
    )
    gate_in = gate_in + jnp.dot(encoded, pick_time, preferred_element_type=jnp.float32)
    gate_hid = jnp.dot(self_full, pick_hidden, preferred_element_type=jnp.float32)
    gate_in, gate_hid = (gate_in, gate_hid)
    ids = asked.reshape(-1)
    mean = node_means(ids, gate_in)
    hidden = own_rows.reshape(total, width_part)
    gx = (mean + bias_input[None, :]).reshape(total, width_part, 3)
    gh = (gate_hid + bias_hidden[None, :]).reshape(total, width_part, 3)
    reset = jax.nn.sigmoid(gx[:, :, 0] + gh[:, :, 0])
    keep = jax.nn.sigmoid(gx[:, :, 1] + gh[:, :, 1])
    cand = jnp.tanh(gx[:, :, 2] + reset * gh[:, :, 2])
    fresh = (1.0 - keep) * cand + keep * hidden
    updated = mem_rows.at[ids].set(fresh, mode="drop")
    return updated.T


def solution(mesh):
    placed = (
        P("cols", "rows"),
        P("rows"),
        P("rows", None),
        P("rows", None),
        P("rows", None),
        P("rows", None),
        P(),
        P(),
        P("cols", None, None),
        P("cols", None),
        P("cols", None),
        P("cols"),
        P("cols"),
    )
    return jax.shard_map(
        local, mesh=mesh, in_specs=placed, out_specs=P("cols", "rows"), check_vma=False
    )
```

profile of v0, /device:TPU:0, one launch (start us, length us, event | category | flops | bytes accessed | tf_op | source)
XLA Modules:
  0.0 234.6 jit_solution(14819838133150528476)
XLA Ops:
  1.4 5.2 %all-to-all-start = ((s32[8,1,256]{2,1,0:T(1,128)}), s32[8,1,256]{2,1,0:T(1,128)S(1)}, u32[]{:S(2)}, u32[]{:S(2)}) async-start(s32[8,1,256]{2,1,0:T(1,128)} %all_to_all.22), calls=%async_computation | async-start | bytes 16384 | tf_op jit(solution)/shard_map/all_to_all | solution.py:51
  7.9 15.4 %all_gather.18 = bf16[128,384]{1,0:T(8,128)(2,1)} all-gather(bf16[32,384]{1,0:T(8,128)(2,1)} %param.24), channel_id=1, replica_groups=mesh['rows'=8,'cols'=4] {'cols'}, dimensions={0}, use_global_device_ids=true | all-gather | bytes 122880 | tf_op jit(solution)/shard_map/all_gather | solution.py:59
  23.3 14.2 %all_gather.16 = bf16[128,2,384]{2,1,0:T(2,128)(2,1)S(1)} all-gather(bf16[32,2,384]{2,1,0:T(2,128)(2,1)} %param.23), channel_id=1, replica_groups=mesh['rows'=8,'cols'=4] {'cols'}, dimensions={0}, use_global_device_ids=true | all-gather | bytes 245760 | tf_op jit(solution)/shard_map/all_gather | solution.py:58
  37.8 13.4 %all_gather.19 = bf16[128,384]{1,0:T(8,128)(2,1)S(1)} all-gather(bf16[32,384]{1,0:T(8,128)(2,1)} %param.25), channel_id=1, replica_groups=mesh['rows'=8,'cols'=4] {'cols'}, dimensions={0}, use_global_device_ids=true | all-gather | bytes 122880 | tf_op jit(solution)/shard_map/all_gather | solution.py:60
  55.3 10.3 %copy.60 = f32[32,32768]{0,1:T(8,128)} copy(f32[32,32768]{1,0:T(8,128)} %param.15) | data formatting | bytes 8388608 | tf_op args[0]
  65.7 3.9 %all-to-all-start.3 = ((s32[8,1,256]{2,1,0:T(1,128)}), s32[8,1,256]{2,1,0:T(1,128)}, u32[]{:S(2)}, u32[]{:S(2)}) async-start(s32[8,1,256]{2,1,0:T(1,128)} %all_to_all.27), calls=%async_computation.3 | async-start | bytes 16384 | tf_op jit(solution)/shard_map/all_to_all | solution.py:52
  70.3 11.2 %gather_fusion = f32[2048,32]{1,0:T(8,128)S(1)} fusion(f32[32768,32]{1,0:T(8,128)} %bitcast.63, s32[2048]{0:T(1024)S(1)} %broadcast_clamp_fusion.1), kind=kCustom, calls=%fused_computation | custom fusion | bytes 532480 | tf_op jit(solution)/shard_map/gather | solution.py:55
  81.8 15.5 %all_gather.15 = bf16[2048,128]{0,1:T(8,128)(2,1)S(1)} all-gather(bf16[2048,32]{0,1:T(8,128)(2,1)S(1)} %copy.61), channel_id=1, replica_groups=mesh['rows'=8,'cols'=4] {'cols'}, dimensions={1}, use_global_device_ids=true | all-gather | bytes 655360 | tf_op jit(solution)/shard_map/all_gather | solution.py:73
  102.4 11.8 %gather_fusion.2 = s32[2048]{0:T(1024)S(1)} fusion(s32[32768]{0:T(1024)S(1)} %copy-done, s32[2048]{0:T(1024)S(1)} %broadcast_clamp_fusion.1), kind=kCustom, calls=%fused_computation.2 | custom fusion | bytes 24576 | tf_op jit(solution)/shard_map/gather | solution.py:56
  115.0 3.9 %all-to-all-start.1 = ((bf16[8,256,32]{1,2,0:T(8,128)(2,1)}), bf16[8,256,32]{1,2,0:T(8,128)(2,1)S(1)}, u32[]{:S(2)}, u32[]{:S(2)}) async-start(bf16[8,256,32]{1,2,0:T(8,128)(2,1)} %copy.63), calls=%async_computation.1 | async-start | bytes 262144 | tf_op jit(solution)/shard_map/all_to_all | solution.py:67
  119.6 4.8 %all-to-all-done.1 = bf16[8,256,32]{1,2,0:T(8,128)(2,1)S(1)} async-done(((bf16[8,256,32]{1,2,0:T(8,128)(2,1)}), bf16[8,256,32]{1,2,0:T(8,128)(2,1)S(1)}, u32[]{:S(2)}, u32[]{:S(2)}) %all-to-all-start.1) | async-done | bytes 131104 | tf_op jit(solution)/shard_map/all_to_all | solution.py:67
  124.7 6.2 %gather_fusion.1 = bf16[2048,32]{1,0:T(8,128)(2,1)S(1)} fusion(bf16[2048,32]{1,0:T(8,128)(2,1)S(1)} %bitcast.66, s32[2048]{0:T(1024)S(1)} %copy-done.4), kind=kCustom, calls=%fused_computation.1 | custom fusion | bytes 270336 | tf_op jit(solution)/shard_map/gather | solution.py:71
  131.8 3.4 %all-to-all-start.2 = ((bf16[8,256,32]{1,2,0:T(8,128)(2,1)}), bf16[8,256,32]{1,2,0:T(8,128)(2,1)S(1)}, u32[]{:S(2)}, u32[]{:S(2)}) async-start(bf16[8,256,32]{1,2,0:T(8,128)(2,1)} %copy.65), calls=%async_computation.2 | async-start | bytes 262144 | tf_op jit(solution)/shard_map/all_to_all | solution.py:72
  135.2 4.6 %fusion.31 = f32[2048,96]{0,1:T(8,128)S(1)} fusion(f32[128]{0:T(128)S(1)} %copy-done.7, f32[128]{0:T(128)S(1)} %copy-done.8, f32[2048]{0:T(1024)S(1)} %subtract_convert_fusion, bf16[128,384]{1,0:T(8,128)(2,1)} %all_gather.18, s32[]{:T(128)S(6)} %select_n.46), kind=kOutput, calls=%fused_computation.36 | convolution fusion | flops 51118080 | bytes 828420 | tf_op jit(solution)/shard_map/dot_general | solution.py:84
  143.8 16.4 %all_gather.17 = bf16[2048,128]{0,1:T(8,128)(2,1)S(1)} all-gather(bf16[2048,32]{0,1:T(8,128)(2,1)S(1)} %bitcast.71), channel_id=1, replica_groups=mesh['rows'=8,'cols'=4] {'cols'}, dimensions={1}, use_global_device_ids=true | all-gather | bytes 655360 | tf_op jit(solution)/shard_map/all_gather | solution.py:76
  161.6 36.7 %while.10 = (s32[]{:T(128)}, f32[4,512,96]{1,0,2:T(4,128)}, s32[4]{0:T(128)S(1)}, s32[2048]{0:T(1024)S(1)}, s32[8,256]{1,0:T(8,128)S(1)}, /*index=5*/f32[2048,96...) while((s32[]{:T(128)}, f32[4,512,96]{1,0,2:T(4,128)}, s32[4]{0:T(128)S(1)}, s32[2048]{0:T(1024)S(1)}, ...), condition=%wide.region_2.3_spmd, body=%wide.region_0.2_spmd.sunk | while | flops 1212202496 | bytes 1814703 | solution.py:23
  163.5 2.2 fusion.56
  165.9 4.9 %dynamic_update_slice.5 = f32[4,512,96]{1,0,2:T(4,128)} dynamic-update-slice(f32[4,512,96]{1,0,2:T(4,128)} %get-tuple-element.133, f32[1,512,96]{1,0,2:T(1,128)S(1)} %copy.92, s32[]{:T(128)S(6)} %copy.96, s32[]{:T(128)} %constant.5.clone.1..sunk, s32[]{:T(128)} %constant.5.clone.1..sunk) | dynamic-update-slice | bytes 393220 | tf_op jit(solution)/shard_map/while/body/jit(dynamic_update_index_in_dim)/dynamic_update_slice | solution.py:23
  175.1 4.9 %dynamic_update_slice.5 = f32[4,512,96]{1,0,2:T(4,128)} dynamic-update-slice(f32[4,512,96]{1,0,2:T(4,128)} %get-tuple-element.133, f32[1,512,96]{1,0,2:T(1,128)S(1)} %copy.92, s32[]{:T(128)S(6)} %copy.96, s32[]{:T(128)} %constant.5.clone.1..sunk, s32[]{:T(128)} %constant.5.clone.1..sunk) | dynamic-update-slice | bytes 393220 | tf_op jit(solution)/shard_map/while/body/jit(dynamic_update_index_in_dim)/dynamic_update_slice | solution.py:23
  184.3 4.9 %dynamic_update_slice.5 = f32[4,512,96]{1,0,2:T(4,128)} dynamic-update-slice(f32[4,512,96]{1,0,2:T(4,128)} %get-tuple-element.133, f32[1,512,96]{1,0,2:T(1,128)S(1)} %copy.92, s32[]{:T(128)S(6)} %copy.96, s32[]{:T(128)} %constant.5.clone.1..sunk, s32[]{:T(128)} %constant.5.clone.1..sunk) | dynamic-update-slice | bytes 393220 | tf_op jit(solution)/shard_map/while/body/jit(dynamic_update_index_in_dim)/dynamic_update_slice | solution.py:23
  193.4 4.9 %dynamic_update_slice.5 = f32[4,512,96]{1,0,2:T(4,128)} dynamic-update-slice(f32[4,512,96]{1,0,2:T(4,128)} %get-tuple-element.133, f32[1,512,96]{1,0,2:T(1,128)S(1)} %copy.92, s32[]{:T(128)S(6)} %copy.96, s32[]{:T(128)} %constant.5.clone.1..sunk, s32[]{:T(128)} %constant.5.clone.1..sunk) | dynamic-update-slice | bytes 393220 | tf_op jit(solution)/shard_map/while/body/jit(dynamic_update_index_in_dim)/dynamic_update_slice | solution.py:23
  200.2 2.2 copy.70
  204.5 18.5 %scatter_custom_fusion = f32[32768,32]{1,0:T(8,128)} fusion(f32[32768,32]{1,0:T(8,128)} %bitcast.64, s32[2048]{0:T(1024)} %bitcast.81, f32[2048,32]{1,0:T(8,128)} %copy-done.1, f32[2048,32,1]{1,0,2:T(8,128)} %copy.81, f32[2048,32,3]{1,0,2:T(8,128)S(1)} %broadcast_add_fusion, f32[2048,32,1]{1,0,2:T(8,128)} %copy.83, f32[2048,32,1]{1,0,2:T(8,128)} %copy.82, ...), kind=kCustom, calls=%fused_computation.31 | custom fusion | flops 917504 | bytes 9176064 | tf_op jit(solution)/shard_map/scatter | solution.py:96
  223.0 11.6 %copy.74 = f32[32,32768]{1,0:T(8,128)} copy(f32[32,32768]{0,1:T(8,128)} %bitcast.65) | data formatting | bytes 8388608 | tf_op jit(solution)/shard_map/transpose | solution.py:97
  (80 shorter events, 37.4 us)
Async XLA Ops:
  0.0 102.4 %copy-start = (s32[32768]{0:T(1024)S(1)}, s32[32768]{0:T(1024)}, u32[]{:S(2)}) copy-start(s32[32768]{0:T(1024)} %param.16) | copy-start | bytes 393220
  1.4 64.3 %all-to-all-start = ((s32[8,1,256]{2,1,0:T(1,128)}), s32[8,1,256]{2,1,0:T(1,128)S(1)}, u32[]{:S(2)}, u32[]{:S(2)}) async-start(s32[8,1,256]{2,1,0:T(1,128)} %all_to_all.22), calls=%async_computation | async-start | bytes 16384 | tf_op jit(solution)/shard_map/all_to_all | solution.py:51
  65.7 49.4 %all-to-all-start.3 = ((s32[8,1,256]{2,1,0:T(1,128)}), s32[8,1,256]{2,1,0:T(1,128)}, u32[]{:S(2)}, u32[]{:S(2)}) async-start(s32[8,1,256]{2,1,0:T(1,128)} %all_to_all.27), calls=%async_computation.3 | async-start | bytes 16384 | tf_op jit(solution)/shard_map/all_to_all | solution.py:52
  70.3 27.0 %copy-start.6 = (f32[96]{0:T(128)S(1)}, f32[96]{0:T(128)}, u32[]{:S(2)}) copy-start(f32[96]{0:T(128)} %param.27) | copy-start | bytes 1156
  81.5 20.8 %copy-start.1 = (f32[2048,32]{1,0:T(8,128)}, f32[2048,32]{1,0:T(8,128)S(1)}, u32[]{:S(2)}) copy-start(f32[2048,32]{1,0:T(8,128)S(1)} %gather_fusion) | copy-start | bytes 786436
  102.4 22.4 %copy-start.4 = (s32[2048]{0:T(1024)S(1)}, s32[2048]{0:T(1024)}, u32[]{:S(2)}) copy-start(s32[2048]{0:T(1024)} %broadcast_clamp_fusion) | copy-start | bytes 24580
  114.2 21.0 %copy-start.7 = (f32[128]{0:T(128)S(1)}, f32[128]{0:T(128)}, u32[]{:S(2)}) copy-start(f32[128]{0:T(128)} %param.22) | copy-start | bytes 1540
  114.2 21.0 %copy-start.8 = (f32[128]{0:T(128)S(1)}, f32[128]{0:T(128)}, u32[]{:S(2)}) copy-start(f32[128]{0:T(128)} %param.21) | copy-start | bytes 1540
  114.2 25.5 %copy-start.3 = (f32[2048,32,1]{0,2,1:T(1,128)S(1)}, f32[2048,32,1]{0,2,1:T(1,128)}, u32[]{:S(2)}) copy-start(f32[2048,32,1]{0,2,1:T(1,128)} %get-tuple-element.80) | copy-start | bytes 786436
  115.0 9.4 %all-to-all-start.1 = ((bf16[8,256,32]{1,2,0:T(8,128)(2,1)}), bf16[8,256,32]{1,2,0:T(8,128)(2,1)S(1)}, u32[]{:S(2)}, u32[]{:S(2)}) async-start(bf16[8,256,32]{1,2,0:T(8,128)(2,1)} %copy.63), calls=%async_computation.1 | async-start | bytes 262144 | tf_op jit(solution)/shard_map/all_to_all | solution.py:67
  119.6 21.5 %copy-start.2 = (f32[2048,32,1]{0,2,1:T(1,128)S(1)}, f32[2048,32,1]{0,2,1:T(1,128)}, u32[]{:S(2)}) copy-start(f32[2048,32,1]{0,2,1:T(1,128)} %get-tuple-element.81) | copy-start | bytes 786436
  131.8 12.0 %all-to-all-start.2 = ((bf16[8,256,32]{1,2,0:T(8,128)(2,1)}), bf16[8,256,32]{1,2,0:T(8,128)(2,1)S(1)}, u32[]{:S(2)}, u32[]{:S(2)}) async-start(bf16[8,256,32]{1,2,0:T(8,128)(2,1)} %copy.65), calls=%async_computation.2 | async-start | bytes 262144 | tf_op jit(solution)/shard_map/all_to_all | solution.py:72
  198.3 4.1 %copy-start.5 = (f32[32,3]{0,1:T(4,128)S(1)}, f32[32,3]{0,1:T(4,128)}, u32[]{:S(2)}) copy-start(f32[32,3]{0,1:T(4,128)} %copy.69) | copy-start | bytes 1156
where the time goes:
time: 236 us; the launch traced here: 235 us
  local copies, waits for them, and re-layouts  93.2 us (39%)
  blocking collectives  74.9 us (32%)
  other arithmetic  25.6 us (11%)
  matrix products  16.7 us (7%)
  starting transfers between devices  16.4 us (7%)
  waiting for transfers between devices  4.8 us (2%)
  loops' own time  2.71 us (1%)
    dynamic_update_slice x8, local copies, waits for them, and re-layouts, node_means(): blocks_out = lax.map(one_block, jnp.arange(turns, dtype=jnp.int32))  20.3 us
    scatter x1, other arithmetic, local(): updated = mem_rows.at[ids].set(fresh, mode='drop')  18.5 us
    unnamed x26, local copies, waits for them, and re-layouts  16.5 us
    all_gather x1, blocking collectives, local(): lax.all_gather(arrived.reshape(total, width_part), 'cols', axis=1, tiled=...  16.4 us
    all_gather x1, blocking collectives, local(): lax.all_gather(own_rows.reshape(total, width_part).astype(jnp.bfloat16),...  15.5 us
    all_gather x1, blocking collectives, local(): lax.all_gather(w_time, 'cols', axis=0, tiled=True)  15.4 us
    all_gather x1, blocking collectives, local(): lax.all_gather(w_pair, 'cols', axis=0, tiled=True)  14.2 us
    all_gather x1, blocking collectives, local(): lax.all_gather(w_hidden, 'cols', axis=0, tiled=True)  13.4 us
  transfers between devices with their start and end apart: 4, of which 1 were waited for; matrix products, arithmetic and copies ran while one was open for 23% of the time, Pallas kernels for 0%

commit v1 on v0

v1 whole, which is shorter than its diff:
```python
import functools

import jax
import jax.numpy as jnp
from jax import lax
from jax.experimental import pallas as pl
from jax.experimental.pallas import tpu as pltpu
from jax.sharding import PartitionSpec as P

MESH = pl.DeviceIdType.MESH
LANES = 128
VM = pl.BlockSpec(memory_space=pltpu.VMEM)
SM = pl.BlockSpec(memory_space=pltpu.SMEM)
ANY = pl.BlockSpec(memory_space=pl.ANY)


def greet(axis, n):
    barrier = pltpu.get_barrier_semaphore()
    me = lax.axis_index(axis)
    for k in range(1, n):
        pl.semaphore_signal(
            barrier, inc=1, device_id={axis: lax.rem(me + k, n)}, device_id_type=MESH
        )


def exchange(axis, n, src, dst, send, recv):
    me = lax.axis_index(axis)
    copies = []
    for k in range(1, n):
        peer = lax.rem(me + k, n)
        copies.append(
            pltpu.make_async_remote_copy(
                src_ref=src.at[peer],
                dst_ref=dst.at[me],
                send_sem=send.at[k],
                recv_sem=recv.at[k],
                device_id={axis: peer},
                device_id_type=MESH,
            )
        )
    for copy in copies:
        copy.start()
    return copies


def first_kernel(n, c, meta, w, meta_out, w_out, ssem, rsem, wssem, wrsem):
    greet("rows", n)
    greet("cols", c)
    pl.semaphore_wait(pltpu.get_barrier_semaphore(), n + c - 2)
    copies = exchange("rows", n, meta, meta_out, ssem, rsem)
    copies += exchange("cols", c, w, w_out, wssem, wrsem)
    row, col = lax.axis_index("rows"), lax.axis_index("cols")
    meta_out[row] = meta[row]
    w_out[col] = w[col]
    for copy in copies:
        copy.wait()


def reply_kernel(n, src, dst, ssem, rsem):
    greet("rows", n)
    pl.semaphore_wait(pltpu.get_barrier_semaphore(), n - 1)
    copies = exchange("rows", n, src, dst, ssem, rsem)
    row = lax.axis_index("rows")
    dst[row] = src[row]
    for copy in copies:
        copy.wait()


def spread_kernel(
    n, c, perm, own, self_all, part_all, own_sem, ssem, rsem, sls, slr, srs, srr, pls, plr, prs, prr
):
    row, col = lax.axis_index("rows"), lax.axis_index("cols")
    barrier = pltpu.get_barrier_semaphore()
    greet("rows", n)
    greet("cols", c)
    pl.semaphore_wait(barrier, n + c - 2)

    def hop(src, dst, send, recv, to):
        return pltpu.make_async_remote_copy(
            src_ref=src,
            dst_ref=dst,
            send_sem=send,
            recv_sem=recv,
            device_id={"cols": to},
            device_id_type=MESH,
        )

    first = pltpu.make_async_copy(perm.at[row], part_all.at[col, row], own_sem.at[0])
    first.start()
    copies = []
    for k in range(1, n):
        peer = lax.rem(row + k, n)
        copies.append(
            pltpu.make_async_remote_copy(
                src_ref=perm.at[peer],
                dst_ref=part_all.at[col, row],
                send_sem=ssem.at[k],
                recv_sem=rsem.at[k],
                device_id={"rows": peer},
                device_id_type=MESH,
            )
        )
    for copy in copies:
        copy.start()
    second = pltpu.make_async_copy(own, self_all.at[col], own_sem.at[1])
    second.start()

    def self_hop(source, t, right):
        sem_s, sem_r = (srs, srr) if right else (sls, slr)
        ref = self_all.at[source]
        src = own if t == 0 else ref
        return hop(src, ref, sem_s.at[t], sem_r.at[t], col + 1 if right else col - 1)

    def part_hop(source, place, t, k, right):
        sem_s, sem_r = (prs, prr) if right else (pls, plr)
        ref = part_all.at[source, place]
        return hop(ref, ref, sem_s.at[t, k], sem_r.at[t, k], col + 1 if right else col - 1)

    can = {True: lambda: col < c - 1, False: lambda: col > 0}
    for right in (True, False):

        @pl.when(can[right]())
        def _(right=right):
            self_hop(col, 0, right).start()

    first.wait()
    for k in range(n):
        place = lax.rem(row - k + n, n)
        if k:
            copies[k - 1].wait_recv()
        for right in (True, False):

            @pl.when(can[right]())
            def _(right=right, k=k, place=place):
                part_hop(col, place, 0, k, right).start()

    for t in range(1, c):
        for right in (True, False):
            source = col - t if right else col + t
            there = source >= 0 if right else source < c
            onward = jnp.logical_and(there, can[right]())

            @pl.when(there)
            def _(right=right, t=t, source=source):
                self_hop(source, t - 1, right).wait_recv()

            @pl.when(onward)
            def _(right=right, t=t, source=source):
                self_hop(source, t, right).start()

        for k in range(n):
            place = lax.rem(row - k + n, n)
            for right in (True, False):
                source = col - t if right else col + t
                there = source >= 0 if right else source < c
                onward = jnp.logical_and(there, can[right]())

                @pl.when(there)
                def _(right=right, t=t, source=source, k=k, place=place):
                    part_hop(source, place, t - 1, k, right).wait_recv()

                @pl.when(onward)
                def _(right=right, t=t, source=source, k=k, place=place):
                    part_hop(source, place, t, k, right).start()

    second.wait()
    for copy in copies:
        copy.wait_send()
    for t in range(c - 1):
        for right in (True, False):
            source = col - t if right else col + t
            there = source >= 0 if right else source < c
            onward = jnp.logical_and(there, can[right]())

            @pl.when(onward)
            def _(right=right, t=t, source=source):
                self_hop(source, t, right).wait_send()
                for k in range(n):
                    part_hop(source, lax.rem(row - k + n, n), t, k, right).wait_send()


def gather_kernel(ids, ticks, memory, last, own, own16, gaps):
    wp, node_rows = memory.shape
    cap = ids.shape[1]
    per = cap // LANES
    lane = lax.broadcasted_iota(jnp.int32, (wp, LANES), 1)
    lane1 = lax.broadcasted_iota(jnp.int32, (1, LANES), 1)

    def tile(i, _):
        block, half = i // per, lax.rem(i, per)

        def slot(j, carry):
            acc, tacc = carry
            node = jnp.minimum(ids[block, half * LANES + j], node_rows - 1)
            t = lax.shift_right_logical(node, 7)
            shift = lax.bitwise_and(j - lax.bitwise_and(node, LANES - 1), LANES - 1)
            x = memory[:, pl.ds(pl.multiple_of(t * LANES, LANES), LANES)]
            acc = jnp.where(lane == j, pltpu.roll(x, shift, 1), acc)
            y = last[pl.ds(t, 1), :]
            tacc = jnp.where(lane1 == j, pltpu.roll(y, shift, 1), tacc)
            return acc, tacc

        zero = (jnp.zeros((wp, LANES), jnp.float32), jnp.zeros((1, LANES), jnp.int32))
        acc, tacc = lax.fori_loop(0, LANES, slot, zero, unroll=16)
        own[:, pl.ds(pl.multiple_of(i * LANES, LANES), LANES)] = acc
        own16[block, :, pl.ds(pl.multiple_of(half * LANES, LANES), LANES)] = acc.astype(
            jnp.bfloat16
        )
        gaps[pl.ds(i, 1), :] = (ticks[pl.ds(i, 1), :] - tacc).astype(jnp.float32)
        return 0

    lax.fori_loop(0, ids.shape[0] * per, tile, 0)


def permute_kernel(held, pair, out, wide):
    n, wp, cap = held.shape
    per = cap // LANES
    tiles = n * per
    for k in range(tiles):
        wide[k] = held[k // per, :, (k % per) * LANES : (k % per + 1) * LANES].astype(jnp.float32)

    def tile(i, _):
        p = pair[pl.ds(i, 1), :]
        where = jnp.broadcast_to(lax.shift_right_logical(p, 7), (8, LANES))
        lane = jnp.broadcast_to(lax.bitwise_and(p, LANES - 1), (8, LANES))
        parts = [jnp.zeros((8, LANES), jnp.float32) for _ in range(wp // 8)]
        for k in range(tiles):
            hit = where == k
            for r in range(wp // 8):
                got = jnp.take_along_axis(wide[k, r * 8 : (r + 1) * 8, :], lane, axis=1)
                parts[r] = jnp.where(hit, got, parts[r])
        whole = jnp.concatenate(parts, axis=0).astype(jnp.bfloat16)
        block, half = i // per, lax.rem(i, per)
        out[block, :, pl.ds(pl.multiple_of(half * LANES, LANES), LANES)] = whole
        return 0

    lax.fori_loop(0, tiles, tile, 0)


def update_kernel(
    ids,
    idrow,
    gaps,
    w,
    bias,
    timing,
    self_all,
    part_all,
    own,
    memory,
    out,
    sem,
    gate_parts,
    gate_hid,
    equal,
    columns,
    fresh,
):
    c, n, wp, cap = self_all.shape
    node_rows = memory.shape[1]
    per = cap // LANES
    tiles = n * per
    g3 = 3 * wp
    load = pltpu.make_async_copy(memory, out, sem)
    load.start()

    from_col = lax.broadcasted_iota(jnp.int32, (g3, g3), 0)
    to_col = lax.broadcasted_iota(jnp.int32, (g3, g3), 1)
    gate, feature = to_col // wp, lax.rem(to_col, wp)
    order = (from_col == 3 * feature + gate).astype(jnp.float32).astype(jnp.bfloat16)

    def weights(kind):
        rows = w[:, kind].reshape(c * wp, g3)
        return jnp.dot(rows, order, preferred_element_type=jnp.float32).astype(jnp.bfloat16)

    w_self, w_part, w_time, w_hid = (weights(k) for k in range(4))
    over_in = (((0,), (0,)), ((), ()))

    def mm(a, b):
        return lax.dot_general(a, b, over_in, preferred_element_type=jnp.float32)

    gate_parts[2 * g3 :, :] = jnp.ones((gate_parts.shape[0] - 2 * g3, n * cap), jnp.bfloat16)

    def chunk(b, _):
        lanes = pl.ds(pl.multiple_of(b * cap, cap), cap)
        xs = self_all[:, b].reshape(c * wp, cap)
        xp = part_all[:, b].reshape(c * wp, cap)
        gap = jnp.concatenate([gaps[pl.ds(b * per + h, 1), :] for h in range(per)], axis=1)
        encoded = jnp.cos(gap * timing[:, 0:1] + timing[:, 1:2]).astype(jnp.bfloat16)
        gi = mm(w_self, xs) + mm(w_part, xp) + mm(w_time, encoded)
        gate_hid[:, lanes] = mm(w_hid, xs) + bias[:, 1:2]
        high = gi.astype(jnp.bfloat16)
        gate_parts[0:g3, lanes] = high
        gate_parts[g3 : 2 * g3, lanes] = (gi - high.astype(jnp.float32)).astype(jnp.bfloat16)
        return 0

    lax.fori_loop(0, n, chunk, 0)

    def column(i, _):
        row = jnp.broadcast_to(idrow[pl.ds(i, 1), :], (LANES, LANES))
        columns[pl.ds(pl.multiple_of(i * LANES, LANES), LANES), :] = row.T
        return 0

    lax.fori_loop(0, tiles, column, 0)

    def means(b, _):
        lanes = pl.ds(pl.multiple_of(b * cap, cap), cap)
        for h in range(per):
            row = idrow[pl.ds(b * per + h, 1), :]
            same = (columns[...] == row).astype(jnp.float32).astype(jnp.bfloat16)
            equal[:, h * LANES : (h + 1) * LANES] = same
        sums = jnp.dot(gate_parts[...], equal[...], preferred_element_type=jnp.float32)
        mean = (sums[0:g3] + sums[g3 : 2 * g3]) / sums[2 * g3 : 2 * g3 + 1]
        gx = mean + bias[:, 0:1]
        gh = gate_hid[:, lanes]
        reset = jax.nn.sigmoid(gx[0:wp] + gh[0:wp])
        keep = jax.nn.sigmoid(gx[wp : 2 * wp] + gh[wp : 2 * wp])
        cand = jnp.tanh(gx[2 * wp :] + reset * gh[2 * wp :])
        fresh[:, lanes] = (1.0 - keep) * cand + keep * own[:, lanes]
        return 0

    lax.fori_loop(0, n, means, 0)
    load.wait()
    lane = lax.broadcasted_iota(jnp.int32, (wp, LANES), 1)

    def tile(i, _):
        block, half = i // per, lax.rem(i, per)
        value = fresh[:, pl.ds(pl.multiple_of(i * LANES, LANES), LANES)]

        def slot(j, _):
            node = ids[block, half * LANES + j]
            safe = jnp.minimum(node, node_rows - 1)
            t = lax.shift_right_logical(safe, 7)
            place = lax.bitwise_and(node, LANES - 1)
            shift = lax.bitwise_and(place - j, LANES - 1)
            place = jnp.where(node < node_rows, place, LANES)
            pltpu.store(
                out.at[:, pl.ds(pl.multiple_of(t * LANES, LANES), LANES)],
                pltpu.roll(value, shift, 1),
                mask=lane == place,
            )
            return 0

        lax.fori_loop(0, LANES, slot, 0, unroll=16)
        return 0

    lax.fori_loop(0, tiles, tile, 0)


def comm(collective):
    return pltpu.CompilerParams(collective_id=collective, has_side_effects=True)


def dma(*shape):
    return pltpu.SemaphoreType.DMA(shape)


def local(
    n,
    c,
    memory,
    last_tick,
    slot_node,
    slot_pair,
    slot_tick,
    block_count,
    time_freq,
    time_phase,
    w_pair,
    w_time,
    w_hidden,
    bias_input,
    bias_hidden,
):
    wp, node_rows = memory.shape
    cap = slot_node.shape[1]
    total = n * cap
    tiles = total // LANES
    g3 = 3 * wp
    f32, i32, b16 = jnp.float32, jnp.int32, jnp.bfloat16
    shape = jax.ShapeDtypeStruct
    block_iota = lax.broadcasted_iota(i32, (n, cap), 0)
    slot_iota = lax.broadcasted_iota(i32, (n, cap), 1)
    filled = slot_iota < block_count.reshape(n, 1)
    local_ids = jnp.where(filled, slot_node - block_iota * node_rows, node_rows)
    meta = jnp.stack([local_ids, slot_tick], axis=1)
    w = jnp.stack([w_pair[:, 0], w_pair[:, 1], w_time, w_hidden], axis=0)
    w = w.reshape(4, wp, c, g3).transpose(2, 0, 1, 3)
    meta, w = pl.pallas_call(
        functools.partial(first_kernel, n, c),
        out_shape=(shape(meta.shape, i32), shape(w.shape, b16)),
        in_specs=[VM, VM],
        out_specs=(VM, VM),
        scratch_shapes=[dma(n), dma(n), dma(c), dma(c)],
        compiler_params=comm(1),
        name="first",
    )(meta, w)
    ids, ticks = meta[:, 0], meta[:, 1].reshape(tiles, LANES)
    own, own16, gaps = pl.pallas_call(
        gather_kernel,
        out_shape=(shape((wp, total), f32), shape((n, wp, cap), b16), shape((tiles, LANES), f32)),
        in_specs=[SM, VM, VM, VM],
        out_specs=(VM, VM, VM),
        name="gather",
    )(ids, ticks, memory, last_tick.reshape(node_rows // LANES, LANES))
    held = pl.pallas_call(
        functools.partial(reply_kernel, n),
        out_shape=shape((n, wp, cap), b16),
        in_specs=[VM],
        out_specs=VM,
        scratch_shapes=[dma(n), dma(n)],
        compiler_params=comm(2),
        name="reply",
    )(own16)
    perm = pl.pallas_call(
        permute_kernel,
        out_shape=shape((n, wp, cap), b16),
        in_specs=[VM, VM],
        out_specs=VM,
        scratch_shapes=[pltpu.VMEM((tiles, wp, LANES), f32)],
        name="permute",
    )(held, slot_pair.reshape(tiles, LANES))
    self_all, part_all = pl.pallas_call(
        functools.partial(spread_kernel, n, c),
        out_shape=(shape((c, n, wp, cap), b16), shape((c, n, wp, cap), b16)),
        in_specs=[VM, VM],
        out_specs=(VM, VM),
        scratch_shapes=[dma(2), dma(n), dma(n)] + [dma(c)] * 4 + [dma(c, n)] * 4,
        compiler_params=comm(3),
        name="spread",
    )(perm, own16)
    bias = jnp.stack(
        [bias_input.reshape(wp, 3).T.reshape(g3), bias_hidden.reshape(wp, 3).T.reshape(g3)], axis=1
    )
    timing = jnp.stack([time_freq, time_phase], axis=1)
    extra = 16
    return pl.pallas_call(
        update_kernel,
        out_shape=shape((wp, node_rows), f32),
        in_specs=[SM] + [VM] * 8 + [ANY],
        out_specs=VM,
        scratch_shapes=[
            pltpu.SemaphoreType.DMA,
            pltpu.VMEM((2 * g3 + extra, total), b16),
            pltpu.VMEM((g3, total), f32),
            pltpu.VMEM((total, cap), b16),
            pltpu.VMEM((total, LANES), f32),
            pltpu.VMEM((wp, total), f32),
        ],
        name="update",
    )(
        ids,
        ids.reshape(tiles, LANES).astype(f32),
        gaps,
        w,
        bias,
        timing,
        self_all,
        part_all,
        own,
        memory,
    )


def solution(mesh):
    placed = (
        P("cols", "rows"),
        P("rows"),
        P("rows", None),
        P("rows", None),
        P("rows", None),
        P("rows", None),
        P(),
        P(),
        P("cols", None, None),
        P("cols", None),
        P("cols", None),
        P("cols"),
        P("cols"),
    )
    return jax.shard_map(
        functools.partial(local, mesh.shape["rows"], mesh.shape["cols"]),
        mesh=mesh,
        in_specs=placed,
        out_specs=P("cols", "rows"),
        check_vma=False,
    )
```

time: 236 us -> 117 us (0.50)
  Pallas kernels: 0 us -> 102 us
  local copies, waits for them, and re-layouts: 93.2 us -> 10.9 us
  blocking collectives: 74.9 us -> 0 us
  other arithmetic: 25.6 us -> 3.36 us
  matrix products: 16.7 us -> 0 us
  starting transfers between devices: 16.4 us -> 0 us
  waiting for transfers between devices: 4.8 us -> 0 us
  loops' own time: 2.71 us -> 0 us
    pallas_call x0 -> x6, Pallas kernels: none -> 102 us  [the longest x1 32.3 us: local(): pl.pallas_call(update_kernel, out_shape=shape((wp, node_rows), f32), in_s...]
    all_gather x5 -> x0, blocking collectives: 74.9 us -> none  [the longest x1 16.4 us: local(): lax.all_gather(arrived.reshape(total, width_part), 'cols', axis=1, tiled=...]
    gather x3 -> x0, local copies, waits for them, and re-layouts: 29.2 us -> none  [the longest x1 11.8 us: local(): own_gaps = (asked_tick - last_tick[safe_ids]).astype(jnp.float32)]
    dynamic_update_slice x8 -> x0, local copies, waits for them, and re-layouts: 20.3 us -> none  [node_means(): blocks_out = lax.map(one_block, jnp.arange(turns, dtype=jnp.int32))]
    scatter x1 -> x0, other arithmetic: 18.5 us -> none  [local(): updated = mem_rows.at[ids].set(fresh, mode='drop')]
    dot_general x8 -> x0, matrix products: 16.7 us -> none  [the longest x4 8.9 us: one_block(): jnp.dot(equal, gate_in, precision=lax.Precision.HIGHEST, preferred_elemen...]
    unnamed x26 -> x0, local copies, waits for them, and re-layouts: 16.5 us -> none
    all_to_all x4 -> x0, starting transfers between devices: 16.4 us -> none  [the longest x1 5.2 us: local(): lax.all_to_all(local_ids, 'rows', split_axis=0, concat_axis=0, tiled=True)]
  transfers between devices with their start and end apart: 4 -> 0, of which waited for: 1 -> 0; matrix products, arithmetic and copies ran while one was open for 23% -> 0% of each run, Pallas kernels for 0% -> 0%
where the time goes in v1:
time: 117 us; the launch traced here: 116 us
  Pallas kernels  102 us (87%)
  local copies, waits for them, and re-layouts  10.9 us (9%)
  other arithmetic  3.36 us (3%)
    pallas_call x1, Pallas kernels, local(): pl.pallas_call(update_kernel, out_shape=shape((wp, node_rows), f32), in_s...  32.3 us
    pallas_call x1, Pallas kernels, local(): pl.pallas_call(functools.partial(spread_kernel, n, c), out_shape=(shape((...  24.6 us
    pallas_call x1, Pallas kernels, local(): pl.pallas_call(gather_kernel, out_shape=(shape((wp, total), f32), shape((...  23.9 us
    pallas_call x1, Pallas kernels, local(): pl.pallas_call(functools.partial(first_kernel, n, c), out_shape=(shape(me...  11.6 us
    pallas_call x1, Pallas kernels, local(): pl.pallas_call(functools.partial(reply_kernel, n), out_shape=shape((n, wp...  6.47 us
    pallas_call x1, Pallas kernels, local(): pl.pallas_call(permute_kernel, out_shape=shape((n, wp, cap), b16), in_spe...  3.33 us

profile of v1, /device:TPU:0, one launch (start us, length us, event | category | flops | bytes accessed | tf_op | source)
XLA Modules:
  0.0 116.5 jit_solution(11158753805390728925)
XLA Ops:
  0.0 0.7 pad_maximum_fusion.1
  0.7 0.8 subtract_select_fusion
  1.5 1.3 %reshape.27.pair = s32[16,128]{1,0:T(8,128)} reshape(s32[8,256]{1,0:T(8,128)} %param.16) | data formatting | bytes 16384 | tf_op jit(solution)/shard_map/reshape | solution.py:422
  2.8 0.7 stack.35
  3.5 0.6 pad_add_fusion.meta
  4.1 0.7 reshape.25
  5.0 0.8 reshape.26
  5.9 0.8 stack.39
  6.8 0.8 stack.40
  7.6 0.7 copy.39.bias
  8.3 1.1 slice_reduce_fusion.1
  9.5 0.1 stack.37
  9.7 0.7 maximum_bitcast_fusion.w
  10.4 11.6 %first.1 = (s32[8,2,256]{2,1,0:T(2,128)}, bf16[4,4,32,96]{3,2,1,0:T(8,128)(2,1)}) custom-call(s32[8,2,256]{2,1,0:T(2,128)} %pad_add_fusion.meta, bf16[4,4,32,96]{3,2,1,0:T(8,128)(2,1)} %maximum_bitcast_fusion.w), custom_call_target="tpu_custom_call" | custom-call | tf_op jit(solution)/shard_map/first/pallas_call | solution.py:389
  21.9 1.3 %slice.15 = s32[8,1,256]{2,1,0:T(1,128)} slice(s32[8,2,256]{2,1,0:T(2,128)} %get-tuple-element.12), slice={[0:8], [1:2], [0:256]} | slice | bytes 16384 | tf_op jit(solution)/shard_map/slice | solution.py:398
  23.3 0.7 copy.36
  24.0 0.6 slice_convert_fusion
  24.6 0.6 convert_element_type.6.idrow
  25.2 0.7 copy.40.timing
  25.9 23.9 %gather.1 = (f32[32,2048]{1,0:T(8,128)}, bf16[8,32,256]{2,1,0:T(8,128)(2,1)}, f32[16,128]{1,0:T(8,128)}) custom-call(s32[8,256]{1,0:T(8,128)} %get-tuple-element.22.ids, s32[16,128]{1,0:T(8,128)} %bitcast.16, f32[32,32768]{1,0:T(8,128)} %memory.3, s32[256,128]{1,0:T(8,128)} %bitcast.13), custom_call_target="tpu_custom_call" | custom-call | tf_op jit(solution)/shard_map/gather/pallas_call | solution.py:399
  49.8 6.5 %reply.1.held = bf16[8,32,256]{2,1,0:T(8,128)(2,1)} custom-call(bf16[8,32,256]{2,1,0:T(8,128)(2,1)} %get-tuple-element.15.src.own), custom_call_target="tpu_custom_call" | custom-call | tf_op jit(solution)/shard_map/reply/pallas_call | solution.py:406
  56.3 3.3 %permute.1.perm = bf16[8,32,256]{2,1,0:T(8,128)(2,1)} custom-call(bf16[8,32,256]{2,1,0:T(8,128)(2,1)} %reply.1.held, s32[16,128]{1,0:T(8,128)} %reshape.27.pair), custom_call_target="tpu_custom_call" | custom-call | tf_op jit(solution)/shard_map/permute/pallas_call | solution.py:415
  59.6 24.6 %spread.1 = (bf16[4,8,32,256]{3,2,1,0:T(8,128)(2,1)}, bf16[4,8,32,256]{3,2,1,0:T(8,128)(2,1)}) custom-call(bf16[8,32,256]{2,1,0:T(8,128)(2,1)} %permute.1.perm, bf16[8,32,256]{2,1,0:T(8,128)(2,1)} %get-tuple-element.15.src.own), custom_call_target="tpu_custom_call" | custom-call | tf_op jit(solution)/shard_map/spread/pallas_call | solution.py:423
  84.2 32.3 %update.1 = f32[32,32768]{1,0:T(8,128)} custom-call(s32[8,256]{1,0:T(8,128)} %get-tuple-element.22.ids, f32[16,128]{1,0:T(8,128)} %convert_element_type.6.idrow, f32[16,128]{1,0:T(8,128)} %get-tuple-element.13.gaps, bf16[4,4,32,96]{3,2,1,0:T(8,128)(2,1)} %get-tuple-element.14.w, f32[96,2]{1,0:T(8,128)} %copy.39.bias, f32[128,2]{1,0:T(8,128)} %copy.40.timing, ...), custom_call_target="tpu_custom_call" | custom-call | tf_op jit(solution)/shard_map/update/pallas_call | solution.py:437
  (12 shorter events, 0.5 us)

commit v2 on v1

v2 whole, which is shorter than its diff:
```python
import functools

import jax
import jax.numpy as jnp
from jax import lax
from jax.experimental import pallas as pl
from jax.experimental.pallas import tpu as pltpu
from jax.sharding import PartitionSpec as P

MESH = pl.DeviceIdType.MESH
LANES = 128
VM = pl.BlockSpec(memory_space=pltpu.VMEM)
SM = pl.BlockSpec(memory_space=pltpu.SMEM)
ANY = pl.BlockSpec(memory_space=pl.ANY)


def greet(axis, n):
    barrier = pltpu.get_barrier_semaphore()
    me = lax.axis_index(axis)
    for k in range(1, n):
        pl.semaphore_signal(
            barrier, inc=1, device_id={axis: lax.rem(me + k, n)}, device_id_type=MESH
        )


def exchange(axis, n, src, dst, send, recv):
    me = lax.axis_index(axis)
    copies = []
    for k in range(1, n):
        peer = lax.rem(me + k, n)
        copies.append(
            pltpu.make_async_remote_copy(
                src_ref=src.at[peer],
                dst_ref=dst.at[me],
                send_sem=send.at[k],
                recv_sem=recv.at[k],
                device_id={axis: peer},
                device_id_type=MESH,
            )
        )
    for copy in copies:
        copy.start()
    return copies


def first_kernel(n, c, meta, w, meta_out, w_out, ssem, rsem, wssem, wrsem):
    greet("rows", n)
    greet("cols", c)
    pl.semaphore_wait(pltpu.get_barrier_semaphore(), n + c - 2)
    copies = exchange("rows", n, meta, meta_out, ssem, rsem)
    copies += exchange("cols", c, w, w_out, wssem, wrsem)
    row, col = lax.axis_index("rows"), lax.axis_index("cols")
    meta_out[row] = meta[row]
    w_out[col] = w[col]
    for copy in copies:
        copy.wait()


def chain(c, block, first, places, sems):
    col = lax.axis_index("cols")
    n = len(places)
    ways = (True, False)

    def hop(source, t, k, right):
        send, recv = sems[0:2] if right else sems[2:4]
        ref = block(source, places[k])
        return pltpu.make_async_remote_copy(
            src_ref=first(k) if t == 0 else ref,
            dst_ref=ref,
            send_sem=send.at[t, k],
            recv_sem=recv.at[t, k],
            device_id={"cols": col + 1 if right else col - 1},
            device_id_type=MESH,
        )

    def goes(right):
        return col < c - 1 if right else col > 0

    def where_from(t, right):
        source = col - t if right else col + t
        there = source >= 0 if right else source < c
        return source, there

    def begin(k):
        for right in ways:

            @pl.when(goes(right))
            def _(right=right):
                hop(col, 0, k, right).start()

    def rest():
        for t in range(1, c):
            for k in range(n):
                for right in ways:
                    source, there = where_from(t, right)

                    @pl.when(there)
                    def _(right=right, source=source, t=t, k=k):
                        hop(source, t - 1, k, right).wait_recv()

                    @pl.when(jnp.logical_and(there, goes(right)))
                    def _(right=right, source=source, t=t, k=k):
                        hop(source, t, k, right).start()

        for t in range(c - 1):
            for right in ways:
                source, there = where_from(t, right)

                @pl.when(jnp.logical_and(there, goes(right)))
                def _(right=right, source=source, t=t):
                    for k in range(n):
                        hop(source, t, k, right).wait_send()

    return begin, rest


def reply_kernel(n, c, src, dst, self_all, ssem, rsem, *sems):
    greet("rows", n)
    greet("cols", c)
    pl.semaphore_wait(pltpu.get_barrier_semaphore(), n + c - 2)
    copies = exchange("rows", n, src, dst, ssem, rsem)
    begin, rest = chain(
        c, lambda source, k: self_all.at[source, k], lambda k: src.at[k], list(range(n)), sems
    )
    for k in range(n):
        begin(k)
    row, col = lax.axis_index("rows"), lax.axis_index("cols")
    dst[row] = src[row]
    self_all[col] = src[...]
    rest()
    for copy in copies:
        copy.wait()


def spread_kernel(n, c, perm, part_all, ssem, rsem, *sems):
    row, col = lax.axis_index("rows"), lax.axis_index("cols")
    greet("rows", n)
    greet("cols", c)
    pl.semaphore_wait(pltpu.get_barrier_semaphore(), n + c - 2)
    copies = []
    for k in range(1, n):
        peer = lax.rem(row + k, n)
        copies.append(
            pltpu.make_async_remote_copy(
                src_ref=perm.at[peer],
                dst_ref=part_all.at[col, row],
                send_sem=ssem.at[k],
                recv_sem=rsem.at[k],
                device_id={"rows": peer},
                device_id_type=MESH,
            )
        )
    for copy in copies:
        copy.start()
    places = [lax.rem(row - k + n, n) for k in range(n)]
    begin, rest = chain(
        c,
        lambda source, place: part_all.at[source, place],
        lambda k: part_all.at[col, places[k]] if k else perm.at[row],
        places,
        sems,
    )
    begin(0)
    part_all[col, row] = perm[row]
    for k in range(1, n):
        copies[k - 1].wait_recv()
        begin(k)
    rest()
    for copy in copies:
        copy.wait_send()


def prepare_kernel(nodes, ticks, counts, w_pair, w_time, w_hid, meta, w, node_rows):
    n, cap = nodes.shape
    c, _, _, g3 = w.shape
    lane = lax.broadcasted_iota(jnp.int32, (1, cap), 1)
    for b in range(n):
        mine = nodes[b : b + 1, :] - b * node_rows
        meta[b, 0:1, :] = jnp.where(lane < counts[0, b], mine, node_rows)
        meta[b, 1:2, :] = ticks[b : b + 1, :]
    width = c * g3
    kinds = (w_pair[:, 0:width], w_pair[:, width : 2 * width], w_time[...], w_hid[...])
    for k, kind in enumerate(kinds):
        for p in range(c):
            w[p, k] = kind[:, p * g3 : (p + 1) * g3]


def load_rows(wp, node_rows, pieces, memory, flat, rows, sems):
    groups = LANES // wp
    step = node_rows // pieces
    copies = []
    for i in range(pieces):
        part = pl.ds(i * step, step)
        copies.append(pltpu.make_async_copy(memory.at[:, part], flat.at[:, part], sems.at[i]))
    for copy in copies:
        copy.start()
    per_piece = step // (groups * LANES)

    def turn(q, _):
        tiles = [
            flat[:, pl.ds(pl.multiple_of((q * groups + k) * LANES, LANES), LANES)]
            for k in range(groups)
        ]
        rows[pl.ds(pl.multiple_of(q * LANES, LANES), LANES), :] = jnp.concatenate(tiles, 0).T
        return 0

    def finish():
        for i, copy in enumerate(copies):
            copy.wait()
            lax.fori_loop(i * per_piece, (i + 1) * per_piece, turn, 0, unroll=4)

    return finish


def row_of(node, groups):
    high = lax.shift_right_logical(node, 7 + groups.bit_length() - 1)
    return high * LANES + lax.bitwise_and(node, LANES - 1)


def gather_kernel(ids, meta, last, memory, own, own16, gaps, flat, rows, picked, tpicked, sems):
    wp, node_rows = memory.shape
    n, _, cap = meta.shape
    per = cap // LANES
    groups = LANES // wp
    finish = load_rows(wp, node_rows, sems.shape[0], memory, flat, rows, sems)
    finish()
    down = lax.broadcasted_iota(jnp.int32, (LANES, LANES), 0)

    def tile(i, _):
        block, half = i // per, lax.rem(i, per)
        lanes = pl.ds(pl.multiple_of(half * LANES, LANES), LANES)

        def slot(j, _):
            node = jnp.minimum(ids[block, 0, half * LANES + j], node_rows - 1)
            picked[pl.ds(j, 1), :] = rows[pl.ds(row_of(node, groups), 1), :]
            tpicked[pl.ds(j, 1), :] = last[pl.ds(lax.shift_right_logical(node, 7), 1), :]
            return 0

        lax.fori_loop(0, LANES, slot, 0, unroll=16)
        node = jnp.minimum(meta[block, 0:1, lanes], node_rows - 1)
        group = lax.bitwise_and(lax.shift_right_logical(node, 7), groups - 1)
        turned = picked[...].T
        mine = turned[0:wp]
        for k in range(1, groups):
            mine = jnp.where(group == k, turned[k * wp : (k + 1) * wp], mine)
        own[:, pl.ds(pl.multiple_of(i * LANES, LANES), LANES)] = mine
        own16[block, :, lanes] = mine.astype(jnp.bfloat16)
        old = tpicked[...].astype(jnp.float32).T
        old = jnp.where(down == lax.bitwise_and(node, LANES - 1), old, 0.0)
        old = jnp.sum(old, axis=0, keepdims=True)
        gaps[pl.ds(i, 1), :] = meta[block, 1:2, lanes].astype(jnp.float32) - old
        return 0

    lax.fori_loop(0, n * per, tile, 0)


def permute_kernel(held, pair, out, wide, flat):
    n, wp, cap = held.shape
    per = cap // LANES
    tiles = n * per
    for k in range(tiles):
        half = slice((k % per) * LANES, (k % per + 1) * LANES)
        flat[k : k + 1, :] = pair[k // per : k // per + 1, half]
        wide[k] = held[k // per, :, (k % per) * LANES : (k % per + 1) * LANES].astype(jnp.float32)

    def tile(block, half):
        p = flat[pl.ds(block * per + half, 1), :]
        where = jnp.broadcast_to(lax.shift_right_logical(p, 7), (8, LANES))
        lane = jnp.broadcast_to(lax.bitwise_and(p, LANES - 1), (8, LANES))
        parts = [jnp.zeros((8, LANES), jnp.float32) for _ in range(wp // 8)]
        for k in range(tiles):
            hit = where == k
            for r in range(wp // 8):
                got = jnp.take_along_axis(wide[k, r * 8 : (r + 1) * 8, :], lane, axis=1)
                parts[r] = jnp.where(hit, got, parts[r])
        whole = jnp.concatenate(parts, axis=0).astype(jnp.bfloat16)
        out[block, :, half * LANES : (half + 1) * LANES] = whole

    def both(block, _):
        for half in range(per):
            tile(block, half)
        return 0

    lax.fori_loop(0, n, both, 0)


def update_kernel(
    ids,
    meta,
    gaps,
    w,
    bias_in,
    bias_hid,
    freq,
    phase,
    self_all,
    part_all,
    own,
    memory,
    out,
    sems,
    out_sems,
    flat,
    rows,
    turned,
    gate_parts,
    gate_hid,
    equal,
    columns,
    fresh,
):
    c, n, wp, cap = self_all.shape
    node_rows = memory.shape[1]
    per = cap // LANES
    tiles = n * per
    g3 = 3 * wp
    groups = LANES // wp
    pieces = sems.shape[0]
    finish = load_rows(wp, node_rows, pieces, memory, flat, rows, sems)

    from_col = lax.broadcasted_iota(jnp.int32, (g3, g3), 0)
    to_col = lax.broadcasted_iota(jnp.int32, (g3, g3), 1)
    gate, feature = to_col // wp, lax.rem(to_col, wp)
    order = (from_col == 3 * feature + gate).astype(jnp.float32).astype(jnp.bfloat16)

    to_row = lax.broadcasted_iota(jnp.int32, (g3, g3), 0)
    hit = lax.broadcasted_iota(jnp.int32, (g3, g3), 1) == 3 * lax.rem(to_row, wp) + to_row // wp
    bias_x, bias_h = (
        jnp.sum(jnp.where(hit, ref[...], 0.0), axis=1, keepdims=True) for ref in (bias_in, bias_hid)
    )
    wide = (freq.shape[1],) * 2
    same_place = lax.broadcasted_iota(jnp.int32, wide, 0) == lax.broadcasted_iota(jnp.int32, wide, 1)
    rate, shift_by = (
        jnp.sum(jnp.where(same_place, ref[...], 0.0), axis=1, keepdims=True) for ref in (freq, phase)
    )

    def weights(kind):
        rows = w[:, kind].reshape(c * wp, g3)
        return jnp.dot(rows, order, preferred_element_type=jnp.float32).astype(jnp.bfloat16)

    w_self, w_part, w_time, w_hid = (weights(k) for k in range(4))
    over_in = (((0,), (0,)), ((), ()))

    def mm(a, b):
        return lax.dot_general(a, b, over_in, preferred_element_type=jnp.float32)

    gate_parts[2 * g3 :, :] = jnp.ones((gate_parts.shape[0] - 2 * g3, n * cap), jnp.bfloat16)

    def chunk(b, _):
        lanes = pl.ds(pl.multiple_of(b * cap, cap), cap)
        xs = self_all[:, b].reshape(c * wp, cap)
        xp = part_all[:, b].reshape(c * wp, cap)
        gap = jnp.concatenate([gaps[pl.ds(b * per + h, 1), :] for h in range(per)], axis=1)
        encoded = jnp.cos(gap * rate + shift_by).astype(jnp.bfloat16)
        gi = mm(w_self, xs) + mm(w_part, xp) + mm(w_time, encoded)
        gate_hid[:, lanes] = mm(w_hid, xs) + bias_h
        high = gi.astype(jnp.bfloat16)
        gate_parts[0:g3, lanes] = high
        gate_parts[g3 : 2 * g3, lanes] = (gi - high.astype(jnp.float32)).astype(jnp.bfloat16)
        return 0

    lax.fori_loop(0, n, chunk, 0)

    def column(i, _):
        lanes = pl.ds(pl.multiple_of(lax.rem(i, per) * LANES, LANES), LANES)
        row = jnp.broadcast_to(meta[i // per, 0:1, lanes].astype(jnp.float32), (LANES, LANES))
        columns[pl.ds(pl.multiple_of(i * LANES, LANES), LANES), :] = row.T
        return 0

    lax.fori_loop(0, tiles, column, 0)

    def means(b, _):
        lanes = pl.ds(pl.multiple_of(b * cap, cap), cap)
        for h in range(per):
            row = meta[b, 0:1, h * LANES : (h + 1) * LANES].astype(jnp.float32)
            same = (columns[...] == row).astype(jnp.float32).astype(jnp.bfloat16)
            equal[:, h * LANES : (h + 1) * LANES] = same
        sums = jnp.dot(gate_parts[...], equal[...], preferred_element_type=jnp.float32)
        mean = (sums[0:g3] + sums[g3 : 2 * g3]) / sums[2 * g3 : 2 * g3 + 1]
        gx = mean + bias_x
        gh = gate_hid[:, lanes]
        reset = jax.nn.sigmoid(gx[0:wp] + gh[0:wp])
        keep = jax.nn.sigmoid(gx[wp : 2 * wp] + gh[wp : 2 * wp])
        cand = jnp.tanh(gx[2 * wp :] + reset * gh[2 * wp :])
        fresh[:, lanes] = (1.0 - keep) * cand + keep * own[:, lanes]
        return 0

    lax.fori_loop(0, n, means, 0)
    finish()
    group_of = lax.broadcasted_iota(jnp.int32, (1, LANES), 1) // wp

    def tile(i, _):
        block, half = i // per, lax.rem(i, per)
        value = fresh[:, pl.ds(pl.multiple_of(i * LANES, LANES), LANES)]
        turned[...] = jnp.concatenate([value] * groups, axis=0).T

        def slot(j, _):
            node = ids[block, 0, half * LANES + j]
            safe = jnp.minimum(node, node_rows - 1)
            group = lax.bitwise_and(lax.shift_right_logical(safe, 7), groups - 1)
            group = jnp.where(node < node_rows, group, groups)
            pltpu.store(
                rows.at[pl.ds(row_of(safe, groups), 1), :],
                turned[pl.ds(j, 1), :],
                mask=group_of == group,
            )
            return 0

        lax.fori_loop(0, LANES, slot, 0, unroll=16)
        return 0

    lax.fori_loop(0, tiles, tile, 0)
    step = node_rows // pieces
    per_piece = step // (groups * LANES)

    def back(q, _):
        x = rows[pl.ds(pl.multiple_of(q * LANES, LANES), LANES), :].T
        for k in range(groups):
            lanes = pl.ds(pl.multiple_of((q * groups + k) * LANES, LANES), LANES)
            flat[:, lanes] = x[k * wp : (k + 1) * wp]
        return 0

    copies = []
    for i in range(pieces):
        lax.fori_loop(i * per_piece, (i + 1) * per_piece, back, 0, unroll=4)
        part = pl.ds(i * step, step)
        copies.append(pltpu.make_async_copy(flat.at[:, part], out.at[:, part], out_sems.at[i]))
        copies[-1].start()
    for copy in copies:
        copy.wait()


def comm(collective):
    return pltpu.CompilerParams(collective_id=collective, has_side_effects=True)


def dma(*shape):
    return pltpu.SemaphoreType.DMA(shape)


def local(
    n,
    c,
    memory,
    last_tick,
    slot_node,
    slot_pair,
    slot_tick,
    block_count,
    time_freq,
    time_phase,
    w_pair,
    w_time,
    w_hidden,
    bias_input,
    bias_hidden,
):
    wp, node_rows = memory.shape
    cap = slot_node.shape[1]
    total = n * cap
    tiles = total // LANES
    g3 = 3 * wp
    f32, i32, b16 = jnp.float32, jnp.int32, jnp.bfloat16
    shape = jax.ShapeDtypeStruct
    pieces = 8
    sent = (shape((n, 2, cap), i32), shape((c, 4, wp, g3), b16))
    meta, w = pl.pallas_call(
        lambda *refs: prepare_kernel(*refs, node_rows),
        out_shape=sent,
        in_specs=[VM, VM, SM, VM, VM, VM],
        out_specs=(VM, VM),
        name="prepare",
    )(slot_node, slot_tick, block_count, w_pair.reshape(wp, 2 * c * g3), w_time, w_hidden)
    meta, w = pl.pallas_call(
        functools.partial(first_kernel, n, c),
        out_shape=(shape(meta.shape, i32), shape(w.shape, b16)),
        in_specs=[VM, VM],
        out_specs=(VM, VM),
        scratch_shapes=[dma(n), dma(n), dma(c), dma(c)],
        compiler_params=comm(1),
        name="first",
    )(meta, w)
    own, own16, gaps = pl.pallas_call(
        gather_kernel,
        out_shape=(shape((wp, total), f32), shape((n, wp, cap), b16), shape((tiles, LANES), f32)),
        in_specs=[SM, VM, VM, ANY],
        out_specs=(VM, VM, VM),
        scratch_shapes=[
            pltpu.VMEM((wp, node_rows), f32),
            pltpu.VMEM((node_rows * wp // LANES, LANES), f32),
            pltpu.VMEM((LANES, LANES), f32),
            pltpu.VMEM((LANES, LANES), i32),
            dma(pieces),
        ],
        name="gather",
    )(meta, meta, last_tick.reshape(node_rows // LANES, LANES), memory)
    everyone = shape((c, n, wp, cap), b16)
    held, self_all = pl.pallas_call(
        functools.partial(reply_kernel, n, c),
        out_shape=(shape((n, wp, cap), b16), everyone),
        in_specs=[VM],
        out_specs=(VM, VM),
        scratch_shapes=[dma(n), dma(n)] + [dma(c, n)] * 4,
        compiler_params=comm(2),
        name="reply",
    )(own16)
    perm = pl.pallas_call(
        permute_kernel,
        out_shape=shape((n, wp, cap), b16),
        in_specs=[VM, VM],
        out_specs=VM,
        scratch_shapes=[pltpu.VMEM((tiles, wp, LANES), f32), pltpu.VMEM((tiles, LANES), i32)],
        name="permute",
    )(held, slot_pair)
    part_all = pl.pallas_call(
        functools.partial(spread_kernel, n, c),
        out_shape=everyone,
        in_specs=[VM],
        out_specs=VM,
        scratch_shapes=[dma(n), dma(n)] + [dma(c, n)] * 4,
        compiler_params=comm(3),
        name="spread",
    )(perm)
    extra = 16
    return pl.pallas_call(
        update_kernel,
        out_shape=shape((wp, node_rows), f32),
        in_specs=[SM] + [VM] * 10 + [ANY],
        out_specs=ANY,
        scratch_shapes=[
            dma(pieces),
            dma(pieces),
            pltpu.VMEM((wp, node_rows), f32),
            pltpu.VMEM((node_rows * wp // LANES, LANES), f32),
            pltpu.VMEM((LANES, LANES), f32),
            pltpu.VMEM((2 * g3 + extra, total), b16),
            pltpu.VMEM((g3, total), f32),
            pltpu.VMEM((total, cap), b16),
            pltpu.VMEM((total, LANES), f32),
            pltpu.VMEM((wp, total), f32),
        ],
        name="update",
    )(
        meta,
        meta,
        gaps,
        w,
        bias_input.reshape(1, g3),
        bias_hidden.reshape(1, g3),
        time_freq.reshape(1, -1),
        time_phase.reshape(1, -1),
        self_all,
        part_all,
        own,
        memory,
    )


def solution(mesh):
    placed = (
        P("cols", "rows"),
        P("rows"),
        P("rows", None),
        P("rows", None),
        P("rows", None),
        P("rows", None),
        P(),
        P(),
        P("cols", None, None),
        P("cols", None),
        P("cols", None),
        P("cols"),
        P("cols"),
    )
    return jax.shard_map(
        functools.partial(local, mesh.shape["rows"], mesh.shape["cols"]),
        mesh=mesh,
        in_specs=placed,
        out_specs=P("cols", "rows"),
        check_vma=False,
    )
```

time: 117 us -> 97.6 us (0.83)
  local copies, waits for them, and re-layouts: 10.9 us -> 1.41 us
  Pallas kernels: 102 us -> 95.8 us
  other arithmetic: 3.36 us -> 0 us
    pallas_call x1, Pallas kernels: 23.9 us -> 16.6 us  [local(): pl.pallas_call(gather_kernel, out_shape=(shape((wp, total), f32), shape((...]
    another operation x14 -> x0, local copies, waits for them, and re-layouts: 4.19 us -> none  [the longest x8 1.86 us: local(): w = jnp.stack([w_pair[:, 0], w_pair[:, 1], w_time, w_hidden], axis=0)]
    pallas_call x2 -> x3, Pallas kernels: 31 us -> 34.8 us  [the longest x1 17.4 us: local(): pl.pallas_call(functools.partial(spread_kernel, n, c), out_shape=everyone...]
    reshape x3 -> x0, local copies, waits for them, and re-layouts: 2.8 us -> none  [the longest x1 1.29 us: local(): slot_pair.reshape(tiles, LANES)]
    slice x2 -> x0, local copies, waits for them, and re-layouts: 2.45 us -> none  [the longest x1 1.32 us: local(): ids, ticks = (meta[:, 0], meta[:, 1].reshape(tiles, LANES))]
    pallas_call x1, Pallas kernels: 32.3 us -> 30 us  [local(): pl.pallas_call(update_kernel, out_shape=shape((wp, node_rows), f32), in_s...]
    unnamed x0 -> x1, local copies, waits for them, and re-layouts: none -> 1.41 us
    another operation x3 -> x0, other arithmetic: 1.3 us -> none  [the longest x1 0.68 us: local(): timing = jnp.stack([time_freq, time_phase], axis=1)]
where the time goes in v2:
time: 97.6 us; the launch traced here: 97.2 us
  Pallas kernels  95.8 us (98%)
  local copies, waits for them, and re-layouts  1.41 us (1%)
    pallas_call x1, Pallas kernels, local(): pl.pallas_call(update_kernel, out_shape=shape((wp, node_rows), f32), in_s...  30 us
    pallas_call x1, Pallas kernels, local(): pl.pallas_call(functools.partial(spread_kernel, n, c), out_shape=everyone...  17.4 us
    pallas_call x1, Pallas kernels, local(): pl.pallas_call(gather_kernel, out_shape=(shape((wp, total), f32), shape((...  16.6 us
    pallas_call x1, Pallas kernels, local(): pl.pallas_call(functools.partial(reply_kernel, n, c), out_shape=(shape((n...  15.7 us
    pallas_call x1, Pallas kernels, local(): pl.pallas_call(functools.partial(first_kernel, n, c), out_shape=(shape(me...  11.6 us
    pallas_call x1, Pallas kernels, local(): pl.pallas_call(permute_kernel, out_shape=shape((n, wp, cap), b16), in_spe...  2.75 us

profile of v2, /device:TPU:0, one launch (start us, length us, event | category | flops | bytes accessed | tf_op | source)
XLA Modules:
  0.0 97.2 jit_solution(14131656311918129214)
XLA Ops:
  0.0 1.4 %copy.14 = bf16[4,8,2,384]{3,1,2,0:T(8,128)(2,1)} copy(bf16[4,8,2,384]{3,2,1,0:T(2,128)(2,1)} %bitcast.9) | data formatting | bytes 98304
  1.4 1.6 %prepare.1 = (s32[8,2,256]{2,1,0:T(2,128)}, bf16[4,4,32,96]{3,2,1,0:T(8,128)(2,1)}) custom-call(s32[8,256]{1,0:T(8,128)} %refs_0_.1, s32[8,256]{1,0:T(8,128)} %refs_1_.1, s32[1,8]{1,0:T(1,128)} %refs_2_.1, bf16[32,768]{1,0:T(8,128)(2,1)} %bitcast.7, bf16[32,384]{1,0:T(8,128)(2,1)} %refs_4_.1, bf16[32,384]{1,0:T(8,128)(2,1)} %refs_5_.1), custom_call_target="tpu_custom_call" | custom-call | tf_op jit(solution)/shard_map/prepare/pallas_call | solution.py:467
  3.1 11.6 %first.1 = (s32[8,2,256]{2,1,0:T(2,128)}, bf16[4,4,32,96]{3,2,1,0:T(8,128)(2,1)}) custom-call(s32[8,2,256]{2,1,0:T(2,128)} %get-tuple-element.14.meta, bf16[4,4,32,96]{3,2,1,0:T(8,128)(2,1)} %get-tuple-element.15.w), custom_call_target="tpu_custom_call" | custom-call | tf_op jit(solution)/shard_map/first/pallas_call | solution.py:474
  14.6 16.6 %gather.1 = (f32[32,2048]{1,0:T(8,128)}, bf16[8,32,256]{2,1,0:T(8,128)(2,1)}, f32[16,128]{1,0:T(8,128)}) custom-call(s32[8,2,256]{2,1,0:T(2,128)} %get-tuple-element.16.ids.meta, s32[8,2,256]{2,1,0:T(2,128)} %get-tuple-element.16.ids.meta, s32[256,128]{1,0:T(8,128)} %bitcast.8, f32[32,32768]{1,0:T(8,128)} %memory.3), custom_call_target="tpu_custom_call" | custom-call | tf_op jit(solution)/shard_map/gather/pallas_call | solution.py:483
  31.3 15.7 %reply.1 = (bf16[8,32,256]{2,1,0:T(8,128)(2,1)}, bf16[4,8,32,256]{3,2,1,0:T(8,128)(2,1)}) custom-call(bf16[8,32,256]{2,1,0:T(8,128)(2,1)} %get-tuple-element.19.src), custom_call_target="tpu_custom_call" | custom-call | tf_op jit(solution)/shard_map/reply/pallas_call | solution.py:498
  47.1 2.8 %permute.1.perm = bf16[8,32,256]{2,1,0:T(8,128)(2,1)} custom-call(bf16[8,32,256]{2,1,0:T(8,128)(2,1)} %get-tuple-element.21.held, s32[8,256]{1,0:T(8,128)} %pair.1), custom_call_target="tpu_custom_call" | custom-call | tf_op jit(solution)/shard_map/permute/pallas_call | solution.py:507
  49.8 17.4 %spread.1.part_all = bf16[4,8,32,256]{3,2,1,0:T(8,128)(2,1)} custom-call(bf16[8,32,256]{2,1,0:T(8,128)(2,1)} %permute.1.perm), custom_call_target="tpu_custom_call" | custom-call | tf_op jit(solution)/shard_map/spread/pallas_call | solution.py:515
  67.2 30.0 %update.1 = f32[32,32768]{1,0:T(8,128)} custom-call(s32[8,2,256]{2,1,0:T(2,128)} %get-tuple-element.16.ids.meta, s32[8,2,256]{2,1,0:T(2,128)} %get-tuple-element.16.ids.meta, f32[16,128]{1,0:T(8,128)} %get-tuple-element.17.gaps, bf16[4,4,32,96]{3,2,1,0:T(8,128)(2,1)} %get-tuple-element.18.w, f32[1,96]{1,0:T(1,128)} %bitcast.10, f32[1,96]{1,0:T(1,128)} %bitcast.11, ...), custom_call_target="tpu_custom_call" | custom-call | tf_op jit(solution)/shard_map/update/pallas_call | solution.py:525
